TPU v7x, 32 devices: a whole 2x2x4 slice. The times are simulated.
32 devices in a mesh: gx: 4 (over x, core), gy: 4 (over z), gz: 2 (over y).
Axes of the slice: x: 2, y: 2, z: 4, core: 2. Of those that a mesh axis runs over, the one named last changes fastest.
Arguments:
- columns: int32 [1024, 2048], P(('gx', 'gy', 'gz')), may hold values from 0 to 32767, as said below
- counts: int32 [1024, 2048], P(('gx', 'gy', 'gz')), may hold values from 1 to 63
- nnz_count: int32 [1024], P(('gx', 'gy', 'gz')), may hold values from 1 to 2048, as said below
- selected: int32 [2048], replicated, may hold values from 0 to 32767, as said below
Outputs:
- gene_stats: float32 [2, 32768], P(None, 'gz')
- pca_input: bfloat16 [1024, 2048], P(('gx', 'gy'), 'gz')
Inputs may be any that keep to these rules, and one draw needn't show every extreme that they name: `columns`: in each row no two slots fall in the same block of 16 consecutive genes (so the first nnz_count slots hold distinct genes); slots beyond nnz_count are not part of the matrix. For every k, the live slots of one cell fall on at most 128 of the genes selected[k * 2048 / 2] to selected[(k + 1) * 2048 / 2 - 1]; some cell reaches 128 for every k in every draw. `nnz_count`: some cell has all 2048 slots live in every draw. `selected`: distinct genes.
All inputs are finite; a program needn't handle non-finite values.
Results may differ from a plain program's by a relative error of at most 0.0085.
Values may be sent and summed in bfloat16 or wider, within the bound.
No kernel may reach another device: no remote copies, remote signals or barrier semaphores. Data moves between devices by JAX's collectives and lax.ppermute only.
A program may use at most 128 MiB of HBM per device.

v0:
```python
import jax
import jax.numpy as jnp
from jax import lax
from jax.sharding import PartitionSpec as P

GENES = 32768
SEL = 2048
target_sum = 10000.0
var_floor = 0.01
clip_value = 10.0
lane_count = 256


def standardize(dense, mean_sel, variance_sel):
    scale_sel = jnp.sqrt(jnp.maximum(variance_sel, var_floor))
    return jnp.clip((dense - mean_sel[None, :]) / scale_sel[None, :], -clip_value, clip_value)


def cell_block(pair):
    block_genes, block_values = pair
    high_count = GENES // lane_count
    high_ids = lax.broadcasted_iota(jnp.int32, (1, 1, high_count), 2)
    low_ids = lax.broadcasted_iota(jnp.int32, (1, 1, lane_count), 2)
    high_table = ((block_genes // lane_count)[:, :, None] == high_ids).astype(jnp.bfloat16)
    low_hit = (block_genes % lane_count)[:, :, None] == low_ids
    upper = lax.optimization_barrier(block_values.astype(jnp.bfloat16))
    lower = (block_values - upper.astype(jnp.float32)).astype(jnp.bfloat16)
    upper_table = jnp.where(low_hit, upper[:, :, None], jnp.bfloat16(0.0))
    lower_table = jnp.where(low_hit, lower[:, :, None], jnp.bfloat16(0.0))
    upper_part = jnp.einsum(
        "csh,csl->chl", high_table, upper_table, preferred_element_type=jnp.float32
    )
    lower_part = jnp.einsum(
        "csh,csl->chl", high_table, lower_table, preferred_element_type=jnp.float32
    )
    return upper_part + lower_part


def per_device(columns, counts, nnz_count, selected):
    local_cells = columns.shape[0]
    row_slots = columns.shape[1]
    owners = lax.axis_size("gz")
    owner_index = lax.axis_index("gz")
    cells = local_cells * lax.axis_size("gx") * lax.axis_size("gy") * owners
    slot = lax.broadcasted_iota(jnp.int32, counts.shape, 1)
    live = slot < nnz_count[:, None]
    raw = jnp.where(live, counts.astype(jnp.float32), jnp.float32(0.0))
    library = jnp.sum(raw, axis=1, keepdims=True)
    values = jnp.log1p(raw * (target_sum / library))
    genes = jnp.where(live, columns, 0)
    block_rows = 4
    block_total = local_cells // block_rows
    expanded = lax.map(
        cell_block,
        (
            genes.reshape(block_total, block_rows, row_slots),
            values.reshape(block_total, block_rows, row_slots),
        ),
    )
    expanded = expanded.reshape(local_cells, GENES)
    total = jnp.sum(expanded, axis=0)
    square = jnp.sum(expanded * expanded, axis=0)
    terms = jnp.stack([total, square])
    owned = GENES // owners
    sums = lax.psum(terms, ("gx", "gy", "gz"))
    own_sums = lax.dynamic_slice_in_dim(sums, owner_index * owned, owned, 1)
    picked_sums = jnp.take(sums, selected, axis=1)
    own_mean = own_sums[0] / cells
    own_variance = own_sums[1] / cells - own_mean * own_mean
    gene_stats = jnp.stack([own_mean, own_variance])
    sel_mean = picked_sums[0] / cells
    sel_variance = picked_sums[1] / cells - sel_mean * sel_mean
    dense = jnp.take(expanded, selected, axis=1)
    share_size = SEL // owners
    own_mean_sel = lax.dynamic_slice_in_dim(sel_mean, owner_index * share_size, share_size, 0)
    own_variance_sel = lax.dynamic_slice_in_dim(
        sel_variance, owner_index * share_size, share_size, 0
    )
    moved = lax.all_to_all(
        dense.astype(jnp.bfloat16), "gz", split_axis=1, concat_axis=0, tiled=True
    ).astype(dense.dtype)
    pca_input = standardize(moved, own_mean_sel, own_variance_sel).astype(jnp.bfloat16)
    return (gene_stats, pca_input)


def solution(mesh):
    return jax.shard_map(
        per_device,
        mesh=mesh,
        in_specs=(
            P(("gx", "gy", "gz"), None),
            P(("gx", "gy", "gz"), None),
            P(("gx", "gy", "gz")),
            P(),
        ),
        out_specs=(P(None, "gz"), P(("gx", "gy"), "gz")),
        check_vma=False,
    )
```

profile of v0, /device:TPU:0, one launch (start us, length us, event | category | flops | bytes accessed | tf_op | source)
XLA Modules:
  0.0 230.8 jit_solution(16225255947262282294)
XLA Ops:
  7.2 1.2 fusion.36
  8.4 1.1 multiply_log-plus-one_fusion
  9.5 0.1 reshape.103
  9.6 1.0 fusion.35
  10.7 0.1 reshape.102
  10.8 56.9 %while.12 = (s32[]{:T(128)}, f32[8,4,128,256]{3,2,1,0:T(8,128)}, s32[8,4,2048]{2,1,0:T(4,128)S(1)}, f32[8,4,2048]{2,1,0:T(4,128)S(1)}, s32[]{:T(128)}) while((s32[]{:T(128)}, f32[8,4,128,256]{3,2,1,0:T(8,128)}, s32[8,4,2048]{2,1,0:T(4,128)S(1)}, f32[8,4,2048]{2,1,0:T(4,128)S(1)}, s32[]{:T(128)}) %tuple.39), condition=%wide.region_2.3_spmd, body=%wide.region_1.2_spmd.sunk | while | flops 1084588032 | bytes 1982553 | solution.py:53
  10.8 0.1 add_select_fusion.4
  10.9 3.2 %fusion.48 = f32[4,128,256]{2,1,0:T(8,128)S(1)} fusion(s32[4,2048]{1,0:T(4,128)S(1)} %add_select_fusion.5, bf16[4,2048]{1,0:T(4,128)(2,1)S(1)} %bitcast_convert_fusion.2, s32[4,2048]{1,0:T(4,128)S(1)} %get-tuple-element.109), kind=kOutput, calls=%fused_computation.5.clone.1 | convolution fusion | flops 542113792 | bytes 606208 | tf_op jit(solution)/shard_map/while/body/eval_jaxpr/csh,csl->chl/dot_general | solution.py:30
  14.1 3.8 %fusion.50 = f32[8,4,128,256]{3,2,1,0:T(8,128)} fusion(f32[8,4,128,256]{3,2,1,0:T(8,128)} %get-tuple-element.116, s32[]{:T(128)S(6)} %copy.30, f32[4,128,256]{2,1,0:T(8,128)S(1)} %fusion.48, s32[4,2048]{1,0:T(4,128)S(1)} %add_select_fusion.5, bf16[4,2048]{1,0:T(4,128)(2,1)S(1)} %fusion.49, s32[4,2048]{1,0:T(4,128)S(1)} %get-tuple-element.109), kind=kOutput, calls=%fused_computation.18.clone.1 | convolution fusion | flops 542244864 | bytes 1130500 | tf_op jit(solution)/shard_map/while/body/eval_jaxpr/csh,csl->chl/dot_general | solution.py:33
  17.9 0.1 add_select_fusion.4
  18.0 3.2 %fusion.48 = f32[4,128,256]{2,1,0:T(8,128)S(1)} fusion(s32[4,2048]{1,0:T(4,128)S(1)} %add_select_fusion.5, bf16[4,2048]{1,0:T(4,128)(2,1)S(1)} %bitcast_convert_fusion.2, s32[4,2048]{1,0:T(4,128)S(1)} %get-tuple-element.109), kind=kOutput, calls=%fused_computation.5.clone.1 | convolution fusion | flops 542113792 | bytes 606208 | tf_op jit(solution)/shard_map/while/body/eval_jaxpr/csh,csl->chl/dot_general | solution.py:30
  21.2 3.8 %fusion.50 = f32[8,4,128,256]{3,2,1,0:T(8,128)} fusion(f32[8,4,128,256]{3,2,1,0:T(8,128)} %get-tuple-element.116, s32[]{:T(128)S(6)} %copy.30, f32[4,128,256]{2,1,0:T(8,128)S(1)} %fusion.48, s32[4,2048]{1,0:T(4,128)S(1)} %add_select_fusion.5, bf16[4,2048]{1,0:T(4,128)(2,1)S(1)} %fusion.49, s32[4,2048]{1,0:T(4,128)S(1)} %get-tuple-element.109), kind=kOutput, calls=%fused_computation.18.clone.1 | convolution fusion | flops 542244864 | bytes 1130500 | tf_op jit(solution)/shard_map/while/body/eval_jaxpr/csh,csl->chl/dot_general | solution.py:33
  25.0 0.1 add_select_fusion.4
  25.1 3.2 %fusion.48 = f32[4,128,256]{2,1,0:T(8,128)S(1)} fusion(s32[4,2048]{1,0:T(4,128)S(1)} %add_select_fusion.5, bf16[4,2048]{1,0:T(4,128)(2,1)S(1)} %bitcast_convert_fusion.2, s32[4,2048]{1,0:T(4,128)S(1)} %get-tuple-element.109), kind=kOutput, calls=%fused_computation.5.clone.1 | convolution fusion | flops 542113792 | bytes 606208 | tf_op jit(solution)/shard_map/while/body/eval_jaxpr/csh,csl->chl/dot_general | solution.py:30
  28.3 3.8 %fusion.50 = f32[8,4,128,256]{3,2,1,0:T(8,128)} fusion(f32[8,4,128,256]{3,2,1,0:T(8,128)} %get-tuple-element.116, s32[]{:T(128)S(6)} %copy.30, f32[4,128,256]{2,1,0:T(8,128)S(1)} %fusion.48, s32[4,2048]{1,0:T(4,128)S(1)} %add_select_fusion.5, bf16[4,2048]{1,0:T(4,128)(2,1)S(1)} %fusion.49, s32[4,2048]{1,0:T(4,128)S(1)} %get-tuple-element.109), kind=kOutput, calls=%fused_computation.18.clone.1 | convolution fusion | flops 542244864 | bytes 1130500 | tf_op jit(solution)/shard_map/while/body/eval_jaxpr/csh,csl->chl/dot_general | solution.py:33
  32.1 0.1 add_select_fusion.4
  32.3 3.2 %fusion.48 = f32[4,128,256]{2,1,0:T(8,128)S(1)} fusion(s32[4,2048]{1,0:T(4,128)S(1)} %add_select_fusion.5, bf16[4,2048]{1,0:T(4,128)(2,1)S(1)} %bitcast_convert_fusion.2, s32[4,2048]{1,0:T(4,128)S(1)} %get-tuple-element.109), kind=kOutput, calls=%fused_computation.5.clone.1 | convolution fusion | flops 542113792 | bytes 606208 | tf_op jit(solution)/shard_map/while/body/eval_jaxpr/csh,csl->chl/dot_general | solution.py:30
  35.4 3.8 %fusion.50 = f32[8,4,128,256]{3,2,1,0:T(8,128)} fusion(f32[8,4,128,256]{3,2,1,0:T(8,128)} %get-tuple-element.116, s32[]{:T(128)S(6)} %copy.30, f32[4,128,256]{2,1,0:T(8,128)S(1)} %fusion.48, s32[4,2048]{1,0:T(4,128)S(1)} %add_select_fusion.5, bf16[4,2048]{1,0:T(4,128)(2,1)S(1)} %fusion.49, s32[4,2048]{1,0:T(4,128)S(1)} %get-tuple-element.109), kind=kOutput, calls=%fused_computation.18.clone.1 | convolution fusion | flops 542244864 | bytes 1130500 | tf_op jit(solution)/shard_map/while/body/eval_jaxpr/csh,csl->chl/dot_general | solution.py:33
  39.3 0.1 add_select_fusion.4
  39.4 3.2 %fusion.48 = f32[4,128,256]{2,1,0:T(8,128)S(1)} fusion(s32[4,2048]{1,0:T(4,128)S(1)} %add_select_fusion.5, bf16[4,2048]{1,0:T(4,128)(2,1)S(1)} %bitcast_convert_fusion.2, s32[4,2048]{1,0:T(4,128)S(1)} %get-tuple-element.109), kind=kOutput, calls=%fused_computation.5.clone.1 | convolution fusion | flops 542113792 | bytes 606208 | tf_op jit(solution)/shard_map/while/body/eval_jaxpr/csh,csl->chl/dot_general | solution.py:30
  42.5 3.8 %fusion.50 = f32[8,4,128,256]{3,2,1,0:T(8,128)} fusion(f32[8,4,128,256]{3,2,1,0:T(8,128)} %get-tuple-element.116, s32[]{:T(128)S(6)} %copy.30, f32[4,128,256]{2,1,0:T(8,128)S(1)} %fusion.48, s32[4,2048]{1,0:T(4,128)S(1)} %add_select_fusion.5, bf16[4,2048]{1,0:T(4,128)(2,1)S(1)} %fusion.49, s32[4,2048]{1,0:T(4,128)S(1)} %get-tuple-element.109), kind=kOutput, calls=%fused_computation.18.clone.1 | convolution fusion | flops 542244864 | bytes 1130500 | tf_op jit(solution)/shard_map/while/body/eval_jaxpr/csh,csl->chl/dot_general | solution.py:33
  46.4 0.1 add_select_fusion.4
  46.5 3.2 %fusion.48 = f32[4,128,256]{2,1,0:T(8,128)S(1)} fusion(s32[4,2048]{1,0:T(4,128)S(1)} %add_select_fusion.5, bf16[4,2048]{1,0:T(4,128)(2,1)S(1)} %bitcast_convert_fusion.2, s32[4,2048]{1,0:T(4,128)S(1)} %get-tuple-element.109), kind=kOutput, calls=%fused_computation.5.clone.1 | convolution fusion | flops 542113792 | bytes 606208 | tf_op jit(solution)/shard_map/while/body/eval_jaxpr/csh,csl->chl/dot_general | solution.py:30
  49.6 3.8 %fusion.50 = f32[8,4,128,256]{3,2,1,0:T(8,128)} fusion(f32[8,4,128,256]{3,2,1,0:T(8,128)} %get-tuple-element.116, s32[]{:T(128)S(6)} %copy.30, f32[4,128,256]{2,1,0:T(8,128)S(1)} %fusion.48, s32[4,2048]{1,0:T(4,128)S(1)} %add_select_fusion.5, bf16[4,2048]{1,0:T(4,128)(2,1)S(1)} %fusion.49, s32[4,2048]{1,0:T(4,128)S(1)} %get-tuple-element.109), kind=kOutput, calls=%fused_computation.18.clone.1 | convolution fusion | flops 542244864 | bytes 1130500 | tf_op jit(solution)/shard_map/while/body/eval_jaxpr/csh,csl->chl/dot_general | solution.py:33
  53.5 0.1 add_select_fusion.4
  53.6 3.2 %fusion.48 = f32[4,128,256]{2,1,0:T(8,128)S(1)} fusion(s32[4,2048]{1,0:T(4,128)S(1)} %add_select_fusion.5, bf16[4,2048]{1,0:T(4,128)(2,1)S(1)} %bitcast_convert_fusion.2, s32[4,2048]{1,0:T(4,128)S(1)} %get-tuple-element.109), kind=kOutput, calls=%fused_computation.5.clone.1 | convolution fusion | flops 542113792 | bytes 606208 | tf_op jit(solution)/shard_map/while/body/eval_jaxpr/csh,csl->chl/dot_general | solution.py:30
  56.7 3.8 %fusion.50 = f32[8,4,128,256]{3,2,1,0:T(8,128)} fusion(f32[8,4,128,256]{3,2,1,0:T(8,128)} %get-tuple-element.116, s32[]{:T(128)S(6)} %copy.30, f32[4,128,256]{2,1,0:T(8,128)S(1)} %fusion.48, s32[4,2048]{1,0:T(4,128)S(1)} %add_select_fusion.5, bf16[4,2048]{1,0:T(4,128)(2,1)S(1)} %fusion.49, s32[4,2048]{1,0:T(4,128)S(1)} %get-tuple-element.109), kind=kOutput, calls=%fused_computation.18.clone.1 | convolution fusion | flops 542244864 | bytes 1130500 | tf_op jit(solution)/shard_map/while/body/eval_jaxpr/csh,csl->chl/dot_general | solution.py:33
  60.7 3.2 %fusion.48 = f32[4,128,256]{2,1,0:T(8,128)S(1)} fusion(s32[4,2048]{1,0:T(4,128)S(1)} %add_select_fusion.5, bf16[4,2048]{1,0:T(4,128)(2,1)S(1)} %bitcast_convert_fusion.2, s32[4,2048]{1,0:T(4,128)S(1)} %get-tuple-element.109), kind=kOutput, calls=%fused_computation.5.clone.1 | convolution fusion | flops 542113792 | bytes 606208 | tf_op jit(solution)/shard_map/while/body/eval_jaxpr/csh,csl->chl/dot_general | solution.py:30
  63.8 3.8 %fusion.50 = f32[8,4,128,256]{3,2,1,0:T(8,128)} fusion(f32[8,4,128,256]{3,2,1,0:T(8,128)} %get-tuple-element.116, s32[]{:T(128)S(6)} %copy.30, f32[4,128,256]{2,1,0:T(8,128)S(1)} %fusion.48, s32[4,2048]{1,0:T(4,128)S(1)} %add_select_fusion.5, bf16[4,2048]{1,0:T(4,128)(2,1)S(1)} %fusion.49, s32[4,2048]{1,0:T(4,128)S(1)} %get-tuple-element.109), kind=kOutput, calls=%fused_computation.18.clone.1 | convolution fusion | flops 542244864 | bytes 1130500 | tf_op jit(solution)/shard_map/while/body/eval_jaxpr/csh,csl->chl/dot_general | solution.py:33
  67.7 2.6 %fusion.39 = (f32[128,256]{1,0:T(8,128)S(1)}, f32[128,256]{1,0:T(8,128)S(1)}) fusion(f32[8,4,128,256]{3,2,1,0:T(8,128)} %get-tuple-element.58), kind=kLoop, calls=%fused_computation.62 | loop fusion | flops 3080192 | bytes 4456448 | tf_op jit(solution)/shard_map/reduce_sum | solution.py:61
  70.3 0.1 copy.24
  70.4 0.1 copy.25
  70.6 0.9 pad_maximum_fusion
  71.6 4.4 %copy.26 = bf16[4,8,128,256]{3,1,2,0:T(8,128)(2,1)S(1)} copy(f32[4,8,128,256]{3,2,1,0:T(8,128)} %bitcast.62) | data formatting | bytes 6291456
  76.0 6.0 %copy.21 = bf16[32,32768]{0,1:T(8,128)(2,1)} copy(bf16[32,32768]{1,0:T(8,128)(2,1)S(1)} %bitcast.63) | data formatting | bytes 4194304 | tf_op jit(solution)/shard_map/reshape | solution.py:60
  82.0 10.1 %gather_fusion = bf16[2048,32]{1,0:T(8,128)(2,1)S(1)} fusion(bf16[32,32768]{0,1:T(8,128)(2,1)} %copy.21, s32[2048]{0:T(1024)S(1)} %fusion.38), kind=kCustom, calls=%fused_computation | custom fusion | bytes 270336 | tf_op jit(solution)/shard_map/jit(_take)/gather | solution.py:73
  92.1 0.2 copy.22
  92.3 0.7 select_convert_fusion
  93.0 4.3 %all-to-all-start = ((bf16[32,2,1024]{2,0,1:T(8,128)(2,1)}), bf16[32,2,1024]{2,0,1:T(8,128)(2,1)S(1)}, u32[]{:S(2)}, u32[]{:S(2)}) async-start(bf16[32,2,1024]{2,0,1:T(8,128)(2,1)} %select_convert_fusion), calls=%async_computation | async-start | bytes 262144 | tf_op jit(solution)/shard_map/all_to_all | solution.py:79
  97.3 103.7 %all-reduce.2.cloned.1.call-done = f32[2,32768]{1,0:T(2,128)} async-done(((f32[2,32768]{1,0:T(2,128)}), f32[2,32768]{1,0:T(2,128)}) %all-reduce.2.cloned.1.call-update) | async-done | bytes 262160 | tf_op jit(solution)/shard_map/psum | solution.py:65
  201.0 8.9 %copy.23 = f32[2,32768]{0,1:T(8,128)} copy(f32[2,32768]{1,0:T(2,128)} %all-reduce.2.cloned.1.call-done) | data formatting | bytes 524288 | tf_op jit(solution)/shard_map/psum | solution.py:65
  209.9 11.2 %gather_fusion.1 = f32[2048,2]{1,0:T(8,128)S(1)} fusion(f32[2,32768]{0,1:T(8,128)} %copy.23, s32[2048]{0:T(1024)S(1)} %fusion.38), kind=kCustom, calls=%fused_computation.1 | custom fusion | bytes 40960 | tf_op jit(solution)/shard_map/jit(_take)/gather | solution.py:67
  221.2 0.3 select_bitcast_fusion
  221.5 0.2 dynamic-slice_multiply_fusion.2
  221.7 0.8 pad_maximum_fusion.1
  222.5 0.3 fusion.40
  222.9 0.4 dynamic-slice_reduce_fusion
  223.2 0.7 fusion.34
  (37 shorter events, 0.6 us)
Async XLA Ops:
  7.2 193.8 %all-reduce.2.cloned.1.call-start = ((), (), s32[]{:S(2)}) async-start(), calls=%async_computation.1 | async-start | bytes 524288 | tf_op jit(solution)/shard_map/psum | solution.py:65
  67.7 3.9 %copy-start.1 = (s32[2048]{0:T(1024)S(1)}, s32[2048]{0:T(1024)}, u32[]{:S(2)}) copy-start(s32[2048]{0:T(1024)} %param.9) | copy-start | bytes 24580
  93.0 130.2 %all-to-all-start = ((bf16[32,2,1024]{2,0,1:T(8,128)(2,1)}), bf16[32,2,1024]{2,0,1:T(8,128)(2,1)S(1)}, u32[]{:S(2)}, u32[]{:S(2)}) async-start(bf16[32,2,1024]{2,0,1:T(8,128)(2,1)} %select_convert_fusion), calls=%async_computation | async-start | bytes 262144 | tf_op jit(solution)/shard_map/all_to_all | solution.py:79
  201.0 20.5 %copy-start = (f32[2,32768]{1,0:T(2,128)S(1)}, f32[2,32768]{1,0:T(2,128)}, u32[]{:S(2)}) copy-start(f32[2,32768]{1,0:T(2,128)} %all-reduce.2.cloned.1.call-done) | copy-start | bytes 786436
Sparse Core Ops, SparseCore 0:
  71.7 129.2 all-reduce.1
where the time goes:
time: 231 us
  waiting for transfers between devices  104 us (45%)
  matrix products  55.7 us (24%)
  local copies, waits for them, and re-layouts  41.3 us (18%)
  between operations  14.2 us (6%)
  other arithmetic  11.3 us (5%)
  starting transfers between devices  4.31 us (2%)
    psum x1, waiting for transfers between devices, per_device(): sums = lax.psum(terms, ('gx', 'gy', 'gz'))  104 us
    dot_general x8, matrix products, cell_block(): jnp.einsum('csh,csl->chl', high_table, lower_table, preferred_element_typ...  30.5 us
    dot_general x8, matrix products, cell_block(): jnp.einsum('csh,csl->chl', high_table, upper_table, preferred_element_typ...  25.2 us
    gather x1, local copies, waits for them, and re-layouts, per_device(): picked_sums = jnp.take(sums, selected, axis=1)  11.2 us
    gather x2, local copies, waits for them, and re-layouts, per_device(): dense = jnp.take(expanded, selected, axis=1)  10.3 us
    psum x1, local copies, waits for them, and re-layouts, per_device(): sums = lax.psum(terms, ('gx', 'gy', 'gz'))  8.92 us
    reshape x1, local copies, waits for them, and re-layouts, per_device(): expanded = expanded.reshape(local_cells, GENES)  5.99 us
    unnamed x7, local copies, waits for them, and re-layouts  4.7 us
  transfers between devices with their start and end apart: 2, of which 1 were waited for; matrix products, arithmetic and copies ran while one was open for 19% of the time, Pallas kernels for 0%

commit v1 on v0

--- a/solution.py
+++ b/solution.py
@@ -1,3 +1,4 @@
+import functools
 import jax
 import jax.numpy as jnp
 from jax import lax
@@ -9,6 +10,13 @@
 var_floor = 0.01
 clip_value = 10.0
 lane_count = 256
+
+
+def name_thing(point, shard_axis, group_axis):
+    return lax.psum(lax.psum(point, shard_axis), group_axis)
+
+
+see_notes = functools.partial(name_thing, shard_axis=("gy", "gz"), group_axis="gx")
 
 
 def standardize(dense, mean_sel, variance_sel):
@@ -62,7 +70,7 @@
     square = jnp.sum(expanded * expanded, axis=0)
     terms = jnp.stack([total, square])
     owned = GENES // owners
-    sums = lax.psum(terms, ("gx", "gy", "gz"))
+    sums = see_notes(terms)
     own_sums = lax.dynamic_slice_in_dim(sums, owner_index * owned, owned, 1)
     picked_sums = jnp.take(sums, selected, axis=1)
     own_mean = own_sums[0] / cells

time: 231 us -> 210 us (0.909)
  waiting for transfers between devices: 104 us -> 82.9 us
    psum x1 -> x2, waiting for transfers between devices: 104 us -> 82.9 us  [name_thing(): return lax.psum(lax.psum(point, shard_axis), group_axis)]
  transfers between devices with their start and end apart: 2 -> 3, of which waited for: 1 -> 2; matrix products, arithmetic and copies ran while one was open for 19% -> 21% of each run, Pallas kernels for 0% -> 0%
where the time goes in v1:
time: 210 us; the launch traced here: 209 us
  waiting for transfers between devices  82.9 us (39%)
  matrix products  55.7 us (27%)
  local copies, waits for them, and re-layouts  41.3 us (20%)
  between operations  14.2 us (7%)
  other arithmetic  11.2 us (5%)
  starting transfers between devices  3.46 us (2%)
    psum x2, waiting for transfers between devices, name_thing(): return lax.psum(lax.psum(point, shard_axis), group_axis)  82.9 us
    dot_general x8, matrix products, cell_block(): jnp.einsum('csh,csl->chl', high_table, lower_table, preferred_element_typ...  30.5 us
    dot_general x8, matrix products, cell_block(): jnp.einsum('csh,csl->chl', high_table, upper_table, preferred_element_typ...  25.2 us
    gather x1, local copies, waits for them, and re-layouts, per_device(): picked_sums = jnp.take(sums, selected, axis=1)  11.2 us
    gather x2, local copies, waits for them, and re-layouts, per_device(): dense = jnp.take(expanded, selected, axis=1)  10.3 us
    psum x1, local copies, waits for them, and re-layouts, name_thing(): return lax.psum(lax.psum(point, shard_axis), group_axis)  8.92 us
    reshape x1, local copies, waits for them, and re-layouts, per_device(): expanded = expanded.reshape(local_cells, GENES)  5.99 us
    unnamed x7, local copies, waits for them, and re-layouts  4.7 us
  transfers between devices with their start and end apart: 3, of which 2 were waited for; matrix products, arithmetic and copies ran while one was open for 21% of the time, Pallas kernels for 0%

profile of v1, /device:TPU:0, one launch (start us, length us, event | category | flops | bytes accessed | tf_op | source)
XLA Modules:
  0.0 209.1 jit_solution(2722997652265311202)
XLA Ops:
  7.2 1.2 fusion.36
  8.4 1.1 multiply_log-plus-one_fusion
  9.5 0.1 reshape.103
  9.6 1.0 fusion.35
  10.7 0.1 reshape.102
  10.8 56.9 %while.12 = (s32[]{:T(128)}, f32[8,4,128,256]{3,2,1,0:T(8,128)}, s32[8,4,2048]{2,1,0:T(4,128)S(1)}, f32[8,4,2048]{2,1,0:T(4,128)S(1)}, s32[]{:T(128)}) while((s32[]{:T(128)}, f32[8,4,128,256]{3,2,1,0:T(8,128)}, s32[8,4,2048]{2,1,0:T(4,128)S(1)}, f32[8,4,2048]{2,1,0:T(4,128)S(1)}, s32[]{:T(128)}) %tuple.39), condition=%wide.region_2.3_spmd, body=%wide.region_1.2_spmd.sunk | while | flops 1084588032 | bytes 1982553 | solution.py:61
  10.8 0.1 add_select_fusion.4
  10.9 3.2 %fusion.48 = f32[4,128,256]{2,1,0:T(8,128)S(1)} fusion(s32[4,2048]{1,0:T(4,128)S(1)} %add_select_fusion.5, bf16[4,2048]{1,0:T(4,128)(2,1)S(1)} %bitcast_convert_fusion.2, s32[4,2048]{1,0:T(4,128)S(1)} %get-tuple-element.109), kind=kOutput, calls=%fused_computation.5.clone.1 | convolution fusion | flops 542113792 | bytes 606208 | tf_op jit(solution)/shard_map/while/body/eval_jaxpr/csh,csl->chl/dot_general | solution.py:38
  14.1 3.8 %fusion.50 = f32[8,4,128,256]{3,2,1,0:T(8,128)} fusion(f32[8,4,128,256]{3,2,1,0:T(8,128)} %get-tuple-element.116, s32[]{:T(128)S(6)} %copy.30, f32[4,128,256]{2,1,0:T(8,128)S(1)} %fusion.48, s32[4,2048]{1,0:T(4,128)S(1)} %add_select_fusion.5, bf16[4,2048]{1,0:T(4,128)(2,1)S(1)} %fusion.49, s32[4,2048]{1,0:T(4,128)S(1)} %get-tuple-element.109), kind=kOutput, calls=%fused_computation.18.clone.1 | convolution fusion | flops 542244864 | bytes 1130500 | tf_op jit(solution)/shard_map/while/body/eval_jaxpr/csh,csl->chl/dot_general | solution.py:41
  17.9 0.1 add_select_fusion.4
  18.0 3.2 %fusion.48 = f32[4,128,256]{2,1,0:T(8,128)S(1)} fusion(s32[4,2048]{1,0:T(4,128)S(1)} %add_select_fusion.5, bf16[4,2048]{1,0:T(4,128)(2,1)S(1)} %bitcast_convert_fusion.2, s32[4,2048]{1,0:T(4,128)S(1)} %get-tuple-element.109), kind=kOutput, calls=%fused_computation.5.clone.1 | convolution fusion | flops 542113792 | bytes 606208 | tf_op jit(solution)/shard_map/while/body/eval_jaxpr/csh,csl->chl/dot_general | solution.py:38
  21.2 3.8 %fusion.50 = f32[8,4,128,256]{3,2,1,0:T(8,128)} fusion(f32[8,4,128,256]{3,2,1,0:T(8,128)} %get-tuple-element.116, s32[]{:T(128)S(6)} %copy.30, f32[4,128,256]{2,1,0:T(8,128)S(1)} %fusion.48, s32[4,2048]{1,0:T(4,128)S(1)} %add_select_fusion.5, bf16[4,2048]{1,0:T(4,128)(2,1)S(1)} %fusion.49, s32[4,2048]{1,0:T(4,128)S(1)} %get-tuple-element.109), kind=kOutput, calls=%fused_computation.18.clone.1 | convolution fusion | flops 542244864 | bytes 1130500 | tf_op jit(solution)/shard_map/while/body/eval_jaxpr/csh,csl->chl/dot_general | solution.py:41
  25.0 0.1 add_select_fusion.4
  25.1 3.2 %fusion.48 = f32[4,128,256]{2,1,0:T(8,128)S(1)} fusion(s32[4,2048]{1,0:T(4,128)S(1)} %add_select_fusion.5, bf16[4,2048]{1,0:T(4,128)(2,1)S(1)} %bitcast_convert_fusion.2, s32[4,2048]{1,0:T(4,128)S(1)} %get-tuple-element.109), kind=kOutput, calls=%fused_computation.5.clone.1 | convolution fusion | flops 542113792 | bytes 606208 | tf_op jit(solution)/shard_map/while/body/eval_jaxpr/csh,csl->chl/dot_general | solution.py:38
  28.3 3.8 %fusion.50 = f32[8,4,128,256]{3,2,1,0:T(8,128)} fusion(f32[8,4,128,256]{3,2,1,0:T(8,128)} %get-tuple-element.116, s32[]{:T(128)S(6)} %copy.30, f32[4,128,256]{2,1,0:T(8,128)S(1)} %fusion.48, s32[4,2048]{1,0:T(4,128)S(1)} %add_select_fusion.5, bf16[4,2048]{1,0:T(4,128)(2,1)S(1)} %fusion.49, s32[4,2048]{1,0:T(4,128)S(1)} %get-tuple-element.109), kind=kOutput, calls=%fused_computation.18.clone.1 | convolution fusion | flops 542244864 | bytes 1130500 | tf_op jit(solution)/shard_map/while/body/eval_jaxpr/csh,csl->chl/dot_general | solution.py:41
  32.1 0.1 add_select_fusion.4
  32.3 3.2 %fusion.48 = f32[4,128,256]{2,1,0:T(8,128)S(1)} fusion(s32[4,2048]{1,0:T(4,128)S(1)} %add_select_fusion.5, bf16[4,2048]{1,0:T(4,128)(2,1)S(1)} %bitcast_convert_fusion.2, s32[4,2048]{1,0:T(4,128)S(1)} %get-tuple-element.109), kind=kOutput, calls=%fused_computation.5.clone.1 | convolution fusion | flops 542113792 | bytes 606208 | tf_op jit(solution)/shard_map/while/body/eval_jaxpr/csh,csl->chl/dot_general | solution.py:38
  35.4 3.8 %fusion.50 = f32[8,4,128,256]{3,2,1,0:T(8,128)} fusion(f32[8,4,128,256]{3,2,1,0:T(8,128)} %get-tuple-element.116, s32[]{:T(128)S(6)} %copy.30, f32[4,128,256]{2,1,0:T(8,128)S(1)} %fusion.48, s32[4,2048]{1,0:T(4,128)S(1)} %add_select_fusion.5, bf16[4,2048]{1,0:T(4,128)(2,1)S(1)} %fusion.49, s32[4,2048]{1,0:T(4,128)S(1)} %get-tuple-element.109), kind=kOutput, calls=%fused_computation.18.clone.1 | convolution fusion | flops 542244864 | bytes 1130500 | tf_op jit(solution)/shard_map/while/body/eval_jaxpr/csh,csl->chl/dot_general | solution.py:41
  39.3 0.1 add_select_fusion.4
  39.4 3.2 %fusion.48 = f32[4,128,256]{2,1,0:T(8,128)S(1)} fusion(s32[4,2048]{1,0:T(4,128)S(1)} %add_select_fusion.5, bf16[4,2048]{1,0:T(4,128)(2,1)S(1)} %bitcast_convert_fusion.2, s32[4,2048]{1,0:T(4,128)S(1)} %get-tuple-element.109), kind=kOutput, calls=%fused_computation.5.clone.1 | convolution fusion | flops 542113792 | bytes 606208 | tf_op jit(solution)/shard_map/while/body/eval_jaxpr/csh,csl->chl/dot_general | solution.py:38
  42.5 3.8 %fusion.50 = f32[8,4,128,256]{3,2,1,0:T(8,128)} fusion(f32[8,4,128,256]{3,2,1,0:T(8,128)} %get-tuple-element.116, s32[]{:T(128)S(6)} %copy.30, f32[4,128,256]{2,1,0:T(8,128)S(1)} %fusion.48, s32[4,2048]{1,0:T(4,128)S(1)} %add_select_fusion.5, bf16[4,2048]{1,0:T(4,128)(2,1)S(1)} %fusion.49, s32[4,2048]{1,0:T(4,128)S(1)} %get-tuple-element.109), kind=kOutput, calls=%fused_computation.18.clone.1 | convolution fusion | flops 542244864 | bytes 1130500 | tf_op jit(solution)/shard_map/while/body/eval_jaxpr/csh,csl->chl/dot_general | solution.py:41
  46.4 0.1 add_select_fusion.4
  46.5 3.2 %fusion.48 = f32[4,128,256]{2,1,0:T(8,128)S(1)} fusion(s32[4,2048]{1,0:T(4,128)S(1)} %add_select_fusion.5, bf16[4,2048]{1,0:T(4,128)(2,1)S(1)} %bitcast_convert_fusion.2, s32[4,2048]{1,0:T(4,128)S(1)} %get-tuple-element.109), kind=kOutput, calls=%fused_computation.5.clone.1 | convolution fusion | flops 542113792 | bytes 606208 | tf_op jit(solution)/shard_map/while/body/eval_jaxpr/csh,csl->chl/dot_general | solution.py:38
  49.6 3.8 %fusion.50 = f32[8,4,128,256]{3,2,1,0:T(8,128)} fusion(f32[8,4,128,256]{3,2,1,0:T(8,128)} %get-tuple-element.116, s32[]{:T(128)S(6)} %copy.30, f32[4,128,256]{2,1,0:T(8,128)S(1)} %fusion.48, s32[4,2048]{1,0:T(4,128)S(1)} %add_select_fusion.5, bf16[4,2048]{1,0:T(4,128)(2,1)S(1)} %fusion.49, s32[4,2048]{1,0:T(4,128)S(1)} %get-tuple-element.109), kind=kOutput, calls=%fused_computation.18.clone.1 | convolution fusion | flops 542244864 | bytes 1130500 | tf_op jit(solution)/shard_map/while/body/eval_jaxpr/csh,csl->chl/dot_general | solution.py:41
  53.6 3.2 %fusion.48 = f32[4,128,256]{2,1,0:T(8,128)S(1)} fusion(s32[4,2048]{1,0:T(4,128)S(1)} %add_select_fusion.5, bf16[4,2048]{1,0:T(4,128)(2,1)S(1)} %bitcast_convert_fusion.2, s32[4,2048]{1,0:T(4,128)S(1)} %get-tuple-element.109), kind=kOutput, calls=%fused_computation.5.clone.1 | convolution fusion | flops 542113792 | bytes 606208 | tf_op jit(solution)/shard_map/while/body/eval_jaxpr/csh,csl->chl/dot_general | solution.py:38
  56.7 3.8 %fusion.50 = f32[8,4,128,256]{3,2,1,0:T(8,128)} fusion(f32[8,4,128,256]{3,2,1,0:T(8,128)} %get-tuple-element.116, s32[]{:T(128)S(6)} %copy.30, f32[4,128,256]{2,1,0:T(8,128)S(1)} %fusion.48, s32[4,2048]{1,0:T(4,128)S(1)} %add_select_fusion.5, bf16[4,2048]{1,0:T(4,128)(2,1)S(1)} %fusion.49, s32[4,2048]{1,0:T(4,128)S(1)} %get-tuple-element.109), kind=kOutput, calls=%fused_computation.18.clone.1 | convolution fusion | flops 542244864 | bytes 1130500 | tf_op jit(solution)/shard_map/while/body/eval_jaxpr/csh,csl->chl/dot_general | solution.py:41
  60.7 3.2 %fusion.48 = f32[4,128,256]{2,1,0:T(8,128)S(1)} fusion(s32[4,2048]{1,0:T(4,128)S(1)} %add_select_fusion.5, bf16[4,2048]{1,0:T(4,128)(2,1)S(1)} %bitcast_convert_fusion.2, s32[4,2048]{1,0:T(4,128)S(1)} %get-tuple-element.109), kind=kOutput, calls=%fused_computation.5.clone.1 | convolution fusion | flops 542113792 | bytes 606208 | tf_op jit(solution)/shard_map/while/body/eval_jaxpr/csh,csl->chl/dot_general | solution.py:38
  63.8 3.8 %fusion.50 = f32[8,4,128,256]{3,2,1,0:T(8,128)} fusion(f32[8,4,128,256]{3,2,1,0:T(8,128)} %get-tuple-element.116, s32[]{:T(128)S(6)} %copy.30, f32[4,128,256]{2,1,0:T(8,128)S(1)} %fusion.48, s32[4,2048]{1,0:T(4,128)S(1)} %add_select_fusion.5, bf16[4,2048]{1,0:T(4,128)(2,1)S(1)} %fusion.49, s32[4,2048]{1,0:T(4,128)S(1)} %get-tuple-element.109), kind=kOutput, calls=%fused_computation.18.clone.1 | convolution fusion | flops 542244864 | bytes 1130500 | tf_op jit(solution)/shard_map/while/body/eval_jaxpr/csh,csl->chl/dot_general | solution.py:41
  67.7 2.6 %fusion.39 = (f32[128,256]{1,0:T(8,128)S(1)}, f32[128,256]{1,0:T(8,128)S(1)}) fusion(f32[8,4,128,256]{3,2,1,0:T(8,128)} %get-tuple-element.58), kind=kLoop, calls=%fused_computation.62 | loop fusion | flops 3080192 | bytes 4456448 | tf_op jit(solution)/shard_map/reduce_sum | solution.py:69
  70.3 0.1 copy.24
  70.4 0.1 copy.25
  70.6 0.9 pad_maximum_fusion
  71.6 4.4 %copy.26 = bf16[4,8,128,256]{3,1,2,0:T(8,128)(2,1)S(1)} copy(f32[4,8,128,256]{3,2,1,0:T(8,128)} %bitcast.62) | data formatting | bytes 6291456
  76.1 6.0 %copy.21 = bf16[32,32768]{0,1:T(8,128)(2,1)} copy(bf16[32,32768]{1,0:T(8,128)(2,1)S(1)} %bitcast.63) | data formatting | bytes 4194304 | tf_op jit(solution)/shard_map/reshape | solution.py:68
  82.1 10.1 %gather_fusion = bf16[2048,32]{1,0:T(8,128)(2,1)S(1)} fusion(bf16[32,32768]{0,1:T(8,128)(2,1)} %copy.21, s32[2048]{0:T(1024)S(1)} %fusion.38), kind=kCustom, calls=%fused_computation | custom fusion | bytes 270336 | tf_op jit(solution)/shard_map/jit(_take)/gather | solution.py:81
  92.1 0.2 copy.22
  92.3 53.1 %all-reduce.3.cloned.1.call-done = f32[2,32768]{1,0:T(2,128)} async-done(((f32[2,32768]{1,0:T(2,128)}), f32[2,32768]{1,0:T(2,128)}) %all-reduce.3.cloned.1.call-update) | async-done | bytes 262160 | tf_op jit(solution)/shard_map/psum | solution.py:16
  145.5 0.7 select_convert_fusion
  146.2 3.4 %all-to-all-start = ((bf16[32,2,1024]{2,0,1:T(8,128)(2,1)}), bf16[32,2,1024]{2,0,1:T(8,128)(2,1)S(1)}, u32[]{:S(2)}, u32[]{:S(2)}) async-start(bf16[32,2,1024]{2,0,1:T(8,128)(2,1)} %select_convert_fusion), calls=%async_computation | async-start | bytes 262144 | tf_op jit(solution)/shard_map/all_to_all | solution.py:87
  149.6 29.7 %all-reduce.5.cloned.1.call-done = f32[2,32768]{1,0:T(2,128)} async-done(((f32[2,32768]{1,0:T(2,128)}), f32[2,32768]{1,0:T(2,128)}) %all-reduce.5.cloned.1.call-update) | async-done | bytes 262160 | tf_op jit(solution)/shard_map/psum | solution.py:16
  179.3 8.9 %copy.23 = f32[2,32768]{0,1:T(8,128)} copy(f32[2,32768]{1,0:T(2,128)} %all-reduce.5.cloned.1.call-done) | data formatting | bytes 524288 | tf_op jit(solution)/shard_map/psum | solution.py:16
  188.2 11.2 %gather_fusion.1 = f32[2048,2]{1,0:T(8,128)S(1)} fusion(f32[2,32768]{0,1:T(8,128)} %copy.23, s32[2048]{0:T(1024)S(1)} %fusion.38), kind=kCustom, calls=%fused_computation.1 | custom fusion | bytes 40960 | tf_op jit(solution)/shard_map/jit(_take)/gather | solution.py:75
  199.5 0.3 select_bitcast_fusion
  199.8 0.2 dynamic-slice_multiply_fusion.2
  200.0 0.8 pad_maximum_fusion.1
  200.8 0.3 fusion.40
  201.2 0.4 dynamic-slice_reduce_fusion
  201.5 0.7 fusion.34
  (40 shorter events, 0.7 us)
Async XLA Ops:
  7.2 138.3 %all-reduce.3.cloned.1.call-start = ((), (), s32[]{:S(2)}) async-start(), calls=%async_computation.1 | async-start | bytes 524288 | tf_op jit(solution)/shard_map/psum | solution.py:16
  67.7 4.0 %copy-start.1 = (s32[2048]{0:T(1024)S(1)}, s32[2048]{0:T(1024)}, u32[]{:S(2)}) copy-start(s32[2048]{0:T(1024)} %param.9) | copy-start | bytes 24580
  71.6 107.7 %all-reduce.5.cloned.1.call-start = ((), (), s32[]{:S(2)}) async-start(), calls=%async_computation.2 | async-start | bytes 524288 | tf_op jit(solution)/shard_map/psum | solution.py:16
  146.2 55.4 %all-to-all-start = ((bf16[32,2,1024]{2,0,1:T(8,128)(2,1)}), bf16[32,2,1024]{2,0,1:T(8,128)(2,1)S(1)}, u32[]{:S(2)}, u32[]{:S(2)}) async-start(bf16[32,2,1024]{2,0,1:T(8,128)(2,1)} %select_convert_fusion), calls=%async_computation | async-start | bytes 262144 | tf_op jit(solution)/shard_map/all_to_all | solution.py:87
  179.3 20.5 %copy-start = (f32[2,32768]{1,0:T(2,128)S(1)}, f32[2,32768]{1,0:T(2,128)}, u32[]{:S(2)}) copy-start(f32[2,32768]{1,0:T(2,128)} %all-reduce.5.cloned.1.call-done) | copy-start | bytes 786436
Sparse Core Ops, SparseCore 0:
  71.7 73.7 all-reduce.2
  147.8 31.4 all-reduce.4
